TPU v7x, 32 devices: a whole 2x2x4 slice. The times are simulated.
32 devices in a mesh: fluid: 8 (over z, y), grp: 4 (over x, core).
Axes of the slice: x: 2, y: 2, z: 4, core: 2. Of those that a mesh axis runs over, the one named last changes fastest.
Arguments:
- acoustic_modes: bfloat16 [262144, 400], P(('fluid', 'grp')), may hold values from -6 to 6
- shell_modes: bfloat16 [8192, 300], P('fluid'), may hold values from -0.0012207031 to 0.0012207031
- wet_counts: int32 [32], P(('fluid', 'grp')), may hold values from 1 to 2048, 26214 in all
- fluid_nodes: int32 [65536], P(('fluid', 'grp')), may hold values from 0 to 8191
- shell_nodes: int32 [65536], P(('fluid', 'grp')), may hold values from 0 to 1023
- wet_area: float32 [65536], P(('fluid', 'grp')), may hold values from 0.15 to 0.6
- shell_freq: float32 [300], replicated, may hold values from 1 to 2
- shell_loss: float32 [300], replicated, may hold values from 0.2 to 0.5
- cavity_freq: float32 [400], replicated, may hold values from 1 to 2
- cavity_loss: float32 [400], replicated, may hold values from 0.2 to 0.5
- freqs: float32 [64], replicated, may hold values from 0.7 to 2.2
- modal_force: float32 [300], replicated, may hold values from -1.5 to 1.5
- cavity_source: float32 [400], replicated, may hold values from -1.5 to 1.5
Outputs:
- pressure: bfloat16 [262144, 128], P(('fluid', 'grp'))
- modal_structure: float32 [2, 64, 300], P(None, 'grp')
Inputs may be any that keep to these rules, and one draw needn't show every extreme that they name: `wet_counts`: slots 0 to count - 1 of a device's 2048 interface slots are live, the others are ignored. `fluid_nodes`: numbered within the device's own 8192 cavity rows. `shell_nodes`: numbered within the 1024 shell rows of the device's fluid index.
All inputs are finite; a program needn't handle non-finite values.
Results may differ from a plain program's by a relative error of at most 0.0055.
Values may be sent and summed in bfloat16 or wider, within the bound.
No kernel may reach another device: no remote copies, remote signals or barrier semaphores. Data moves between devices by JAX's collectives and lax.ppermute only.
A program may use at most 64 MiB of HBM per device.

v0:
```python
import math
import jax
import jax.numpy as jnp
from jax import lax
from jax.sharding import PartitionSpec as P

SECTIONS = 4
HIGH = lax.Precision.HIGHEST


def divide_complex(real_part, imag_part, denom_real, denom_imag):
    scale = denom_real * denom_real + denom_imag * denom_imag
    return (
        (real_part * denom_real + imag_part * denom_imag) / scale,
        (imag_part * denom_real - real_part * denom_imag) / scale,
    )


def modal_terms(omega, loss, freqs):
    stiff = omega * omega
    real_part = stiff[None, :] - (freqs * freqs)[:, None]
    imag_part = jnp.broadcast_to((loss * stiff)[None, :], real_part.shape)
    return (real_part, imag_part)


def couple_rows(shell_modes, wet_rows, node_rows, live_counts):
    depth, width, cavity = wet_rows.shape
    block = math.gcd(depth, 256)
    result = jnp.zeros((shell_modes.shape[1], cavity), jnp.float32)
    source = 0

    def add_block(number, carry, source=source):
        first = number * block
        piece = lax.dynamic_slice(wet_rows, (first, source, 0), (block, 1, cavity)).reshape(
            block, cavity
        )
        picks = lax.dynamic_slice(node_rows, (first, source), (block, 1)).reshape(block)
        shell_rows = shell_modes[picks]
        return carry + lax.dot_general(
            shell_rows, piece, (((0,), (0,)), ((), ())), preferred_element_type=jnp.float32
        )

    result = lax.fori_loop(0, (live_counts[source] + block - 1) // block, add_block, result)
    return result


def on_device(
    acoustic_modes,
    shell_modes,
    wet_counts,
    fluid_nodes,
    shell_nodes,
    wet_area,
    shell_freq,
    shell_loss,
    cavity_freq,
    cavity_loss,
    freqs,
    modal_force,
    cavity_source,
):
    groups = lax.axis_size("grp")
    member = lax.axis_index("grp")
    slots = fluid_nodes.shape[0]
    freq_total = freqs.shape[0]
    freq_count = freq_total // groups
    count = wet_counts[0]
    live = (jnp.arange(slots, dtype=jnp.int32) < count).astype(jnp.float32)
    wet_rows = (
        wet_area[:, None] * acoustic_modes[fluid_nodes].astype(jnp.float32) * live[:, None]
    ).astype(jnp.bfloat16)
    partial_sum = couple_rows(shell_modes, wet_rows[:, None, :], shell_nodes[:, None], [count])
    ds_re, ds_im = modal_terms(shell_freq, shell_loss, freqs)
    da_re, da_im = modal_terms(cavity_freq, cavity_loss, freqs)
    free_re, free_im = divide_complex(
        jnp.broadcast_to(cavity_source[None, :], da_re.shape), jnp.zeros_like(da_re), da_re, da_im
    )
    free_amps = jnp.concatenate([free_re, free_im], 0).astype(jnp.bfloat16)
    free_field = lax.dot_general(
        acoustic_modes, free_amps, (((1,), (1,)), ((), ())), preferred_element_type=jnp.float32
    )
    squared = (freqs * freqs)[:, None]
    coupling = lax.psum(partial_sum, ("fluid", "grp"))
    start = member * freq_count

    def own_rows(values):
        return lax.dynamic_slice_in_dim(values, start, freq_count, 0)

    shell_re, shell_im = (own_rows(ds_re), own_rows(ds_im))
    cavity_re, cavity_im = (own_rows(da_re), own_rows(da_im))
    base_re, base_im = (own_rows(free_re), own_rows(free_im))
    own_squared = own_rows(squared)
    coupled_re = jnp.zeros_like(base_re)
    coupled_im = jnp.zeros_like(base_im)
    for section in range(SECTIONS):
        amounts = jnp.concatenate([base_re + coupled_re, base_im + coupled_im], 0)
        loads = jnp.dot(amounts, coupling.T, precision=HIGH)
        struct_re, struct_im = divide_complex(
            modal_force[None, :] + loads[:freq_count], loads[freq_count:], shell_re, shell_im
        )
        back = jnp.dot(jnp.concatenate([struct_re, struct_im], 0), coupling, precision=HIGH)
        coupled_re, coupled_im = divide_complex(
            own_squared * back[:freq_count], own_squared * back[freq_count:], cavity_re, cavity_im
        )
    mine = jnp.stack([coupled_re, coupled_im]).astype(jnp.bfloat16)
    coupled_amps = lax.all_gather(mine, "grp", axis=1, tiled=True).reshape(2 * freq_total, -1)
    modal_structure = jnp.stack([struct_re, struct_im])
    coupled_field = lax.dot_general(
        acoustic_modes, coupled_amps, (((1,), (1,)), ((), ())), preferred_element_type=jnp.float32
    )
    pressure = (free_field + coupled_field).astype(jnp.bfloat16)
    return (pressure, modal_structure)


def solution(mesh):
    placed = (
        P(("fluid", "grp"), None),
        P("fluid", None),
        P(("fluid", "grp")),
        P(("fluid", "grp")),
        P(("fluid", "grp")),
        P(("fluid", "grp")),
        P(),
        P(),
        P(),
        P(),
        P(),
        P(),
        P(),
    )
    return jax.shard_map(
        on_device,
        mesh=mesh,
        in_specs=placed,
        out_specs=(P(("fluid", "grp"), None), P(None, "grp", None)),
        check_vma=False,
    )
```

profile of v0, /device:TPU:9, one launch (start us, length us, event | category | flops | bytes accessed | tf_op | source)
XLA Modules:
  0.0 214.8 jit_solution(2672962643485708296)
XLA Ops:
  7.9 10.7 %copy.19 = bf16[8192,400]{1,0:T(8,128)(2,1)} copy(bf16[8192,400]{0,1:T(8,128)(2,1)} %param.15) | data formatting | bytes 13107200 | tf_op args[0]
  18.6 12.1 %gather_fusion.1 = bf16[2048,400]{1,0:T(8,128)(2,1)S(1)} fusion(bf16[8192,400]{1,0:T(8,128)(2,1)} %copy.19, s32[2048]{0:T(1024)S(1)} %fusion.69), kind=kCustom, calls=%fused_computation.1 | custom fusion | bytes 3284992 | tf_op jit(solution)/shard_map/gather | solution.py:70
  30.7 1.7 fusion.6
  32.4 2.8 %copy.21 = bf16[2048,1,400]{0,2,1:T(8,128)(2,1)S(1)} copy(bf16[2048,1,400]{2,0,1:T(8,128)(2,1)} %fusion.6) | data formatting | bytes 3276800 | tf_op jit(solution)/shard_map/while | solution.py:43
  35.2 1.4 copy.20
  36.7 17.5 %while.10 = (s32[]{:T(128)}, f32[300,400]{0,1:T(8,128)S(1)}, s32[]{:T(128)}, s32[2048,1]{0,1:T(1,128)}, bf16[1024,300]{1,0:T(8,128)(2,1)S(1)}, /*index=5*/bf16[2...) while((s32[]{:T(128)}, f32[300,400]{0,1:T(8,128)S(1)}, s32[]{:T(128)}, ...), condition=%wide.region_1.2_spmd, body=%wide.region_0.1_spmd.sunk | while | flops 61561796 | bytes 1811355 | solution.py:43
  36.8 0.7 compare_select_fusion.3
  37.5 1.2 gather_fusion
  39.0 0.7 compare_select_fusion.3
  39.7 1.2 gather_fusion
  41.2 0.7 compare_select_fusion.3
  41.8 1.2 gather_fusion
  43.3 0.7 compare_select_fusion.3
  44.0 1.2 gather_fusion
  45.5 0.7 compare_select_fusion.3
  46.2 1.2 gather_fusion
  47.7 0.7 compare_select_fusion.3
  48.4 1.2 gather_fusion
  50.6 1.2 gather_fusion
  52.1 0.7 compare_select_fusion.3
  52.8 1.2 gather_fusion
  54.3 0.8 copy-done.1
  55.4 6.2 %fusion.12 = f32[128,8192]{1,0:T(8,128)} fusion(bf16[8192,400]{0,1:T(8,128)(2,1)} %param.15, bf16[64,400]{1,0:T(8,128)(2,1)S(1)} %get-tuple-element.88, bf16[64,400]{1,0:T(8,128)(2,1)S(1)} %get-tuple-element.85), kind=kOutput, calls=%fused_computation.22 | convolution fusion | flops 839065600 | bytes 10850304 | tf_op jit(solution)/shard_map/dot_general | solution.py:79
  61.6 120.4 %all-reduce.2.cloned.1.call-done = f32[300,400]{0,1:T(8,128)} async-done(((f32[300,400]{0,1:T(8,128)}), f32[300,400]{0,1:T(8,128)}) %all-reduce.2.cloned.1.call-update) | async-done | bytes 480016 | tf_op jit(solution)/shard_map/psum | solution.py:83
  182.1 1.7 fusion.16
  183.8 1.8 fusion.32
  185.7 1.5 fusion.20
  187.3 1.8 fusion.36
  189.1 1.5 fusion.24
  192.8 7.9 %all_gather.3 = bf16[2,64,400]{2,1,0:T(8,128)(2,1)S(1)} all-gather(bf16[2,16,400]{2,1,0:T(8,128)(2,1)S(1)} %pad_maximum_fusion.1), channel_id=1, replica_groups=mesh['fluid'=8,'grp'=4] {'grp'}, dimensions={1}, use_global_device_ids=true | all-gather | bytes 128000 | tf_op jit(solution)/shard_map/all_gather | solution.py:106
  200.7 4.1 %fusion.4 = bf16[8192,128]{0,1:T(8,128)(2,1)S(1)} fusion(f32[128,8192]{1,0:T(8,128)S(1)} %copy-done.2, bf16[128,400]{1,0:T(8,128)(2,1)S(1)} %bitcast.38, bf16[8192,400]{0,1:T(8,128)(2,1)} %param.15), kind=kOutput, calls=%fused_computation.10 | convolution fusion | flops 840957952 | bytes 12947456 | tf_op jit(solution)/shard_map/dot_general | solution.py:108
  204.9 2.4 %copy.22 = bf16[8192,128]{1,0:T(8,128)(2,1)} copy(bf16[8192,128]{0,1:T(8,128)(2,1)S(1)} %fusion.4) | data formatting | bytes 4194304
  (65 shorter events, 6.7 us)
Async XLA Ops:
  7.2 174.9 %all-reduce.2.cloned.1.call-start = ((), (), s32[]{:S(2)}) async-start(), calls=%async_computation | async-start | bytes 1228800 | tf_op jit(solution)/shard_map/psum | solution.py:83
  7.9 10.7 %copy-start.6 = (s32[2048]{0:T(1024)S(1)}, s32[2048]{0:T(1024)}, u32[]{:S(2)}) copy-start(s32[2048]{0:T(1024)} %param.18) | copy-start | bytes 24580
  18.6 12.1 %copy-start.4 = (f32[2048]{0:T(1024)S(1)}, f32[2048]{0:T(1024)}, u32[]{:S(2)}) copy-start(f32[2048]{0:T(1024)} %param.20) | copy-start | bytes 24580
  36.7 18.4 %copy-start.11 = (f32[64]{0:T(128)S(1)}, f32[64]{0:T(128)}, u32[]{:S(2)}) copy-start(f32[64]{0:T(128)} %param.25) | copy-start | bytes 772
  36.7 18.5 %copy-start.7 = (f32[400]{0:T(512)S(1)}, f32[400]{0:T(512)}, u32[]{:S(2)}) copy-start(f32[400]{0:T(512)} %param.24) | copy-start | bytes 4804
  36.7 18.5 %copy-start.8 = (f32[400]{0:T(512)S(1)}, f32[400]{0:T(512)}, u32[]{:S(2)}) copy-start(f32[400]{0:T(512)} %param.23) | copy-start | bytes 4804
  36.7 18.5 %copy-start.5 = (f32[400]{0:T(512)S(1)}, f32[400]{0:T(512)}, u32[]{:S(2)}) copy-start(f32[400]{0:T(512)} %param.27) | copy-start | bytes 4804
  54.3 0.8 copy-start.1
  55.3 6.3 %copy-start.9 = (f32[300]{0:T(512)S(1)}, f32[300]{0:T(512)}, u32[]{:S(2)}) copy-start(f32[300]{0:T(512)} %param.22) | copy-start | bytes 3604
  55.4 6.3 %copy-start.10 = (f32[300]{0:T(512)S(1)}, f32[300]{0:T(512)}, u32[]{:S(2)}) copy-start(f32[300]{0:T(512)} %param.21) | copy-start | bytes 3604
  55.4 128.3 %copy-start.3 = (f32[300]{0:T(512)S(1)}, f32[300]{0:T(512)}, u32[]{:S(2)}) copy-start(f32[300]{0:T(512)} %param.26) | copy-start | bytes 3604
  182.0 8.7 %copy-start = (f32[300,400]{0,1:T(8,128)S(1)}, f32[300,400]{0,1:T(8,128)}, u32[]{:S(2)}) copy-start(f32[300,400]{0,1:T(8,128)} %all-reduce.2.cloned.1.call-done) | copy-start | bytes 1440004
  182.1 18.7 %copy-start.2 = (f32[128,8192]{1,0:T(8,128)S(1)}, f32[128,8192]{1,0:T(8,128)}, u32[]{:S(2)}) copy-start(f32[128,8192]{1,0:T(8,128)} %fusion.12) | copy-start | bytes 12582916
Sparse Core Ops, SparseCore 0:
  55.2 126.7 all-reduce.1
where the time goes:
time: 216 us; the launch traced here: 215 us
  waiting for transfers between devices  120 us (56%)
  local copies, waits for them, and re-layouts  39.7 us (18%)
  matrix products  22.6 us (10%)
  between operations  15 us (7%)
  other arithmetic  8.73 us (4%)
  blocking collectives  7.9 us (4%)
    psum x1, waiting for transfers between devices, on_device(): coupling = lax.psum(partial_sum, ('fluid', 'grp'))  120 us
    unnamed x26, local copies, waits for them, and re-layouts  14 us
    gather x1, local copies, waits for them, and re-layouts, on_device(): acoustic_modes[fluid_nodes].astype(jnp.float32)  12.1 us
    gather x8, local copies, waits for them, and re-layouts, add_block(): shell_rows = shell_modes[picks]  9.31 us
    all_gather x1, blocking collectives, on_device(): lax.all_gather(mine, 'grp', axis=1, tiled=True).reshape(2 * freq_total, -1)  7.9 us
    dot_general x1, matrix products, on_device(): lax.dot_general(acoustic_modes, free_amps, (((1,), (1,)), ((), ())), pref...  6.15 us
    select_n x8, other arithmetic, add_block(): shell_rows = shell_modes[picks]  5.49 us
    dot_general x4, matrix products, on_device(): loads = jnp.dot(amounts, coupling.T, precision=HIGH)  5.1 us
  transfers between devices with their start and end apart: 1, of which 1 were waited for; matrix products, arithmetic and copies ran while one was open for 3% of the time, Pallas kernels for 0%

commit v1 on v0

--- a/solution.py
+++ b/solution.py
@@ -80,7 +80,9 @@
         acoustic_modes, free_amps, (((1,), (1,)), ((), ())), preferred_element_type=jnp.float32
     )
     squared = (freqs * freqs)[:, None]
-    coupling = lax.psum(partial_sum, ("fluid", "grp"))
+    coupling = partial_sum
+    for mesh_axis in ("grp", "fluid"):
+        coupling = lax.psum(coupling, mesh_axis)
     start = member * freq_count
 
     def own_rows(values):

time: 216 us -> 198 us (0.917)
  waiting for transfers between devices: 120 us -> 102 us
    psum x1 -> x2, waiting for transfers between devices: 120 us -> 102 us  [on_device(): coupling = lax.psum(coupling, mesh_axis)]
  transfers between devices with their start and end apart: 1 -> 2, of which waited for: 1 -> 2; matrix products, arithmetic and copies ran while one was open for 3% -> 3% of each run, Pallas kernels for 0% -> 0%
where the time goes in v1:
time: 198 us; the launch traced here: 196 us
  waiting for transfers between devices  102 us (52%)
  local copies, waits for them, and re-layouts  39.8 us (20%)
  matrix products  22.5 us (11%)
  between operations  15.1 us (8%)
  other arithmetic  8.73 us (4%)
  blocking collectives  7.42 us (4%)
    psum x2, waiting for transfers between devices, on_device(): coupling = lax.psum(coupling, mesh_axis)  102 us
    unnamed x26, local copies, waits for them, and re-layouts  14 us
    gather x1, local copies, waits for them, and re-layouts, on_device(): acoustic_modes[fluid_nodes].astype(jnp.float32)  12.1 us
    gather x8, local copies, waits for them, and re-layouts, add_block(): shell_rows = shell_modes[picks]  9.31 us
    all_gather x1, blocking collectives, on_device(): lax.all_gather(mine, 'grp', axis=1, tiled=True).reshape(2 * freq_total, -1)  7.42 us
    dot_general x1, matrix products, on_device(): lax.dot_general(acoustic_modes, free_amps, (((1,), (1,)), ((), ())), pref...  6.06 us
    select_n x8, other arithmetic, add_block(): shell_rows = shell_modes[picks]  5.49 us
    dot_general x4, matrix products, on_device(): loads = jnp.dot(amounts, coupling.T, precision=HIGH)  5.1 us
  transfers between devices with their start and end apart: 2, of which 2 were waited for; matrix products, arithmetic and copies ran while one was open for 3% of the time, Pallas kernels for 0%

profile of v1, /device:TPU:9, one launch (start us, length us, event | category | flops | bytes accessed | tf_op | source)
XLA Modules:
  0.0 196.0 jit_solution(5997298084784146419)
XLA Ops:
  7.9 10.7 %copy.19 = bf16[8192,400]{1,0:T(8,128)(2,1)} copy(bf16[8192,400]{0,1:T(8,128)(2,1)} %param.15) | data formatting | bytes 13107200 | tf_op args[0]
  18.6 12.1 %gather_fusion.1 = bf16[2048,400]{1,0:T(8,128)(2,1)S(1)} fusion(bf16[8192,400]{1,0:T(8,128)(2,1)} %copy.19, s32[2048]{0:T(1024)S(1)} %fusion.69), kind=kCustom, calls=%fused_computation.1 | custom fusion | bytes 3284992 | tf_op jit(solution)/shard_map/gather | solution.py:70
  30.7 1.7 fusion.6
  32.4 2.8 %copy.21 = bf16[2048,1,400]{0,2,1:T(8,128)(2,1)S(1)} copy(bf16[2048,1,400]{2,0,1:T(8,128)(2,1)} %fusion.6) | data formatting | bytes 3276800 | tf_op jit(solution)/shard_map/while | solution.py:43
  35.2 1.4 copy.20
  36.8 17.5 %while.10 = (s32[]{:T(128)}, f32[300,400]{0,1:T(8,128)S(1)}, s32[]{:T(128)}, s32[2048,1]{0,1:T(1,128)}, bf16[1024,300]{1,0:T(8,128)(2,1)S(1)}, /*index=5*/bf16[2...) while((s32[]{:T(128)}, f32[300,400]{0,1:T(8,128)S(1)}, s32[]{:T(128)}, ...), condition=%wide.region_1.2_spmd, body=%wide.region_0.1_spmd.sunk | while | flops 61561796 | bytes 1811355 | solution.py:43
  36.8 0.7 compare_select_fusion.3
  37.5 1.2 gather_fusion
  39.0 0.7 compare_select_fusion.3
  39.7 1.2 gather_fusion
  41.2 0.7 compare_select_fusion.3
  41.9 1.2 gather_fusion
  43.4 0.7 compare_select_fusion.3
  44.1 1.2 gather_fusion
  45.6 0.7 compare_select_fusion.3
  46.2 1.2 gather_fusion
  47.7 0.7 compare_select_fusion.3
  48.4 1.2 gather_fusion
  50.6 1.2 gather_fusion
  52.8 1.2 gather_fusion
  54.3 0.8 copy-done.1
  55.5 32.0 %all-reduce.3.cloned.1.call-done = f32[300,400]{0,1:T(8,128)} async-done(((f32[300,400]{0,1:T(8,128)}), f32[300,400]{0,1:T(8,128)}) %all-reduce.3.cloned.1.call-update) | async-done | bytes 480016 | tf_op jit(solution)/shard_map/psum | solution.py:85
  87.6 6.1 %fusion.12 = f32[128,8192]{1,0:T(8,128)} fusion(bf16[8192,400]{0,1:T(8,128)(2,1)} %param.15, bf16[64,400]{1,0:T(8,128)(2,1)S(1)} %get-tuple-element.88, bf16[64,400]{1,0:T(8,128)(2,1)S(1)} %get-tuple-element.85), kind=kOutput, calls=%fused_computation.22 | convolution fusion | flops 839065600 | bytes 10850304 | tf_op jit(solution)/shard_map/dot_general | solution.py:79
  93.6 70.1 %all-reduce.5.cloned.1.call-done = f32[300,400]{0,1:T(8,128)} async-done(((f32[300,400]{0,1:T(8,128)}), f32[300,400]{0,1:T(8,128)}) %all-reduce.5.cloned.1.call-update) | async-done | bytes 480016 | tf_op jit(solution)/shard_map/psum | solution.py:85
  163.8 1.7 fusion.16
  165.5 1.8 fusion.32
  167.4 1.5 fusion.20
  169.0 1.8 fusion.36
  170.8 1.5 fusion.24
  174.5 7.4 %all_gather.3 = bf16[2,64,400]{2,1,0:T(8,128)(2,1)S(1)} all-gather(bf16[2,16,400]{2,1,0:T(8,128)(2,1)S(1)} %pad_maximum_fusion.1), channel_id=1, replica_groups=mesh['fluid'=8,'grp'=4] {'grp'}, dimensions={1}, use_global_device_ids=true | all-gather | bytes 128000 | tf_op jit(solution)/shard_map/all_gather | solution.py:108
  182.0 4.1 %fusion.4 = bf16[8192,128]{0,1:T(8,128)(2,1)S(1)} fusion(f32[128,8192]{1,0:T(8,128)S(1)} %copy-done.2, bf16[128,400]{1,0:T(8,128)(2,1)S(1)} %bitcast.38, bf16[8192,400]{0,1:T(8,128)(2,1)} %param.15), kind=kOutput, calls=%fused_computation.10 | convolution fusion | flops 840957952 | bytes 12947456 | tf_op jit(solution)/shard_map/dot_general | solution.py:110
  186.1 2.4 %copy.22 = bf16[8192,128]{1,0:T(8,128)(2,1)} copy(bf16[8192,128]{0,1:T(8,128)(2,1)S(1)} %fusion.4) | data formatting | bytes 4194304
  (68 shorter events, 7.4 us)
Async XLA Ops:
  7.2 80.4 %all-reduce.3.cloned.1.call-start = ((), (), s32[]{:S(2)}) async-start(), calls=%async_computation | async-start | bytes 1228800 | tf_op jit(solution)/shard_map/psum | solution.py:85
  7.9 10.7 %copy-start.6 = (s32[2048]{0:T(1024)S(1)}, s32[2048]{0:T(1024)}, u32[]{:S(2)}) copy-start(s32[2048]{0:T(1024)} %param.18) | copy-start | bytes 24580
  18.6 12.1 %copy-start.4 = (f32[2048]{0:T(1024)S(1)}, f32[2048]{0:T(1024)}, u32[]{:S(2)}) copy-start(f32[2048]{0:T(1024)} %param.20) | copy-start | bytes 24580
  36.7 18.5 %copy-start.11 = (f32[64]{0:T(128)S(1)}, f32[64]{0:T(128)}, u32[]{:S(2)}) copy-start(f32[64]{0:T(128)} %param.25) | copy-start | bytes 772
  36.7 18.5 %copy-start.7 = (f32[400]{0:T(512)S(1)}, f32[400]{0:T(512)}, u32[]{:S(2)}) copy-start(f32[400]{0:T(512)} %param.24) | copy-start | bytes 4804
  36.7 18.5 %copy-start.8 = (f32[400]{0:T(512)S(1)}, f32[400]{0:T(512)}, u32[]{:S(2)}) copy-start(f32[400]{0:T(512)} %param.23) | copy-start | bytes 4804
  36.7 18.5 %copy-start.5 = (f32[400]{0:T(512)S(1)}, f32[400]{0:T(512)}, u32[]{:S(2)}) copy-start(f32[400]{0:T(512)} %param.27) | copy-start | bytes 4804
  36.7 18.8 %copy-start.9 = (f32[300]{0:T(512)S(1)}, f32[300]{0:T(512)}, u32[]{:S(2)}) copy-start(f32[300]{0:T(512)} %param.22) | copy-start | bytes 3604
  36.8 18.8 %copy-start.10 = (f32[300]{0:T(512)S(1)}, f32[300]{0:T(512)}, u32[]{:S(2)}) copy-start(f32[300]{0:T(512)} %param.21) | copy-start | bytes 3604
  54.3 0.8 copy-start.1
  55.2 108.6 %all-reduce.5.cloned.1.call-start = ((), (), s32[]{:S(2)}) async-start(), calls=%async_computation.1 | async-start | bytes 1228800 | tf_op jit(solution)/shard_map/psum | solution.py:85
  87.5 77.9 %copy-start.3 = (f32[300]{0:T(512)S(1)}, f32[300]{0:T(512)}, u32[]{:S(2)}) copy-start(f32[300]{0:T(512)} %param.26) | copy-start | bytes 3604
  163.7 8.7 %copy-start = (f32[300,400]{0,1:T(8,128)S(1)}, f32[300,400]{0,1:T(8,128)}, u32[]{:S(2)}) copy-start(f32[300,400]{0,1:T(8,128)} %all-reduce.5.cloned.1.call-done) | copy-start | bytes 1440004
  163.7 18.2 %copy-start.2 = (f32[128,8192]{1,0:T(8,128)S(1)}, f32[128,8192]{1,0:T(8,128)}, u32[]{:S(2)}) copy-start(f32[128,8192]{1,0:T(8,128)} %fusion.12) | copy-start | bytes 12582916
Sparse Core Ops, SparseCore 0:
  55.3 32.1 all-reduce.2
  91.0 72.7 all-reduce.4
